TPU v7x, 32 devices: a whole 2x2x4 slice. The times are simulated.
32 devices in a mesh: fsdp: 4 (over y, x), ctx: 4 (over z), tp: 2 (over core).
Axes of the slice: x: 2, y: 2, z: 4, core: 2. Of those that a mesh axis runs over, the one named last changes fastest.
Arguments:
- tokens: bfloat16 [8, 1024, 768], P('fsdp', 'ctx'), may hold values from -6 to 6
- lengths: int32 [8], P('fsdp'), may hold values from 256 to 1024, as said below
- cotangent: bfloat16 [8, 1024, 768], P('fsdp', 'ctx'), may hold values from -6 to 6
- ln1_gain: float32 [768], replicated, may hold values from 0.5 to 1.5
- ln1_bias: float32 [768], replicated, may hold values from -1.8 to 1.8
- qkv_weight: bfloat16 [768, 3, 768], P('fsdp', None, 'tp'), may hold values from -0.21875 to 0.21875
- conv_kernel: float32 [3, 3, 768], P(None, None, 'tp'), may hold values from -3.5 to 3.5
- conv_bias: float32 [3, 768], P(None, 'tp'), may hold values from -1.8 to 1.8
- out_weight: bfloat16 [768, 768], P('tp', 'fsdp'), may hold values from -1.75 to 1.75
- ln2_gain: float32 [768], replicated, may hold values from 0.5 to 1.5
- ln2_bias: float32 [768], replicated, may hold values from -1.8 to 1.8
- up_weight: bfloat16 [768, 3072], P('fsdp', 'tp'), may hold values from -0.21875 to 0.21875
- down_weight: bfloat16 [3072, 768], P('tp', 'fsdp'), may hold values from -0.109375 to 0.109375
Outputs:
- result: bfloat16 [8, 1024, 768], P('fsdp', 'ctx')
- input_grad: float32 [8, 1024, 768], P('fsdp', 'ctx')
- ln1_gain_grad: float32 [768], replicated
- ln1_bias_grad: float32 [768], replicated
- qkv_weight_grad: float32 [768, 3, 768], P('fsdp', None, 'tp')
- conv_kernel_grad: float32 [3, 3, 768], P(None, None, 'tp')
- conv_bias_grad: float32 [3, 768], P(None, 'tp')
- out_weight_grad: float32 [768, 768], P('tp', 'fsdp')
- ln2_gain_grad: float32 [768], replicated
- ln2_bias_grad: float32 [768], replicated
- up_weight_grad: float32 [768, 3072], P('fsdp', 'tp')
- down_weight_grad: float32 [3072, 768], P('tp', 'fsdp')
Inputs may be any that keep to these rules, and one draw needn't show every extreme that they name: `lengths`: some slot holds 1024 tokens and some other slot 256.
All inputs are finite; a program needn't handle non-finite values.
Results may differ from a plain program's by a relative error of at most 0.014.
The roundings to bfloat16 on the way count: a program that leaves them out, or rounds other values in their place, can miss the bound.
Values may be sent and summed in bfloat16 or wider, within the bound.
A program may use at most 256 MiB of HBM per device.

v0:
```python
import jax
import jax.numpy as jnp
from jax import lax
from jax.sharding import PartitionSpec as P

HD = 64


EPSILON = 1e-05
SCALING = 0.125
MASKED = -1e30


def shifted(block, axis, distance):
    devices = range(lax.axis_size(axis))
    route = [(i - distance, i) for i in devices if i - distance in devices]
    return lax.ppermute(block, axis, route)


def layer_norm(row_data, norm_gain, shift_bias):
    centred = row_data - jnp.mean(row_data, axis=-1, keepdims=True)
    recip = lax.rsqrt(jnp.mean(centred * centred, axis=-1, keepdims=True) + EPSILON)
    normed = centred * recip
    return (normed * norm_gain + shift_bias, normed, recip)


def norm_back(grad_in, normed, recip, norm_gain):
    scaled = grad_in * norm_gain
    return recip * (
        scaled
        - jnp.mean(scaled, axis=-1, keepdims=True)
        - normed * jnp.mean(scaled * normed, axis=-1, keepdims=True)
    )


def tile_scores(query_part, key_part, query_pos, key_pos, lengths):
    scores = (
        jnp.einsum("mqhd,mkhd->mhqk", query_part, key_part, preferred_element_type=jnp.float32)
        * SCALING
    )
    allowed = (key_pos[None, None, :] <= query_pos[None, :, None]) & (
        key_pos[None, None, :] < lengths[:, None, None]
    )
    return jnp.where(allowed[:, None], scores, MASKED)


def tile_grads(
    query_part, key_part, value_part, grad_part, log_part, delta_part, query_pos, key_pos, lengths
):
    probs_full = jnp.exp(tile_scores(query_part, key_part, query_pos, key_pos, lengths) - log_part)
    prob_grad = jnp.einsum(
        "mqhd,mkhd->mhqk", grad_part, value_part, preferred_element_type=jnp.float32
    )
    score_grad = (probs_full * (prob_grad - delta_part)).astype(jnp.bfloat16)
    return (probs_full, prob_grad, score_grad)


def local(
    tokens,
    lengths,
    cotangent,
    ln1_gain,
    ln1_bias,
    qkv_weight,
    conv_kernel,
    conv_bias,
    out_weight,
    ln2_gain,
    ln2_bias,
    up_weight,
    down_weight,
):
    batches, block_rows, model_width = tokens.shape
    all_rows = batches * block_rows
    qkv_full, out_full, up_full_w, down_full_w = (
        lax.all_gather(qkv_weight, "fsdp", axis=0, tiled=True),
        lax.all_gather(out_weight, "fsdp", axis=1, tiled=True),
        lax.all_gather(up_weight, "fsdp", axis=0, tiled=True),
        lax.all_gather(down_weight, "fsdp", axis=1, tiled=True),
    )
    local_width = qkv_full.shape[2]
    local_heads = local_width // HD
    ctx_count = lax.axis_size("ctx")
    slot_span = block_rows * ctx_count
    group_blocks = 4
    key_span = block_rows * group_blocks
    ctx_index = lax.axis_index("ctx")
    positions = ctx_index * block_rows + jnp.arange(block_rows, dtype=jnp.int32)
    span_iota = jnp.arange(key_span, dtype=jnp.int32)
    block_count = (ctx_index * block_rows + block_rows + key_span - 1) // key_span
    token_valid = positions[None, :] < lengths[:, None]

    def span_slice(array_data, block, axis_pos):
        return lax.dynamic_slice_in_dim(array_data, block * key_span, key_span, axis_pos)

    inputs = tokens.astype(jnp.float32).reshape(all_rows, model_width)
    first_out, first_hat, first_recip = layer_norm(inputs, ln1_gain, ln1_bias)
    first_low = first_out.astype(jnp.bfloat16)
    pre_low = jnp.einsum(
        "td,dcn->tcn", first_low, qkv_full, preferred_element_type=jnp.float32
    ).astype(jnp.bfloat16)
    pre_low = pre_low.reshape(batches, block_rows, 3, local_width)
    earlier = shifted(pre_low[:, block_rows - 2 :], "ctx", 1)
    extended = jnp.concatenate([earlier, pre_low], axis=1).astype(jnp.float32)
    conv_out = (
        conv_bias
        + conv_kernel[0] * extended[:, 2:]
        + conv_kernel[1] * extended[:, 1:-1]
        + conv_kernel[2] * extended[:, :-2]
    ).astype(jnp.bfloat16)
    query_heads = conv_out[:, :, 0].reshape(batches, block_rows, local_heads, HD)
    own_pairs = conv_out[:, :, 1:]
    whole_pairs = lax.all_gather(own_pairs, "ctx", axis=1, tiled=True)
    key_heads = whole_pairs[:, :, 0].reshape(batches, slot_span, local_heads, HD)
    value_heads = whole_pairs[:, :, 1].reshape(batches, slot_span, local_heads, HD)

    def stat_step(block, carry):
        row_max, total = carry
        key_pos = block * key_span + span_iota
        scores = tile_scores(
            query_heads, span_slice(key_heads, block, 1), positions, key_pos, lengths
        )
        new_max = jnp.maximum(row_max, jnp.max(scores, axis=-1, keepdims=True))
        total = total * jnp.exp(row_max - new_max) + jnp.sum(
            jnp.exp(scores - new_max), axis=-1, keepdims=True
        )
        return (new_max, total)

    stat_shape = (batches, local_heads, block_rows, 1)
    row_max, total = lax.fori_loop(
        0,
        block_count,
        stat_step,
        (jnp.full(stat_shape, MASKED, jnp.float32), jnp.zeros(stat_shape, jnp.float32)),
    )
    log_total = row_max + jnp.log(total)

    def value_step(block, accum):
        key_pos = block * key_span + span_iota
        scores = tile_scores(
            query_heads, span_slice(key_heads, block, 1), positions, key_pos, lengths
        )
        probs_low = jnp.exp(scores - log_total).astype(jnp.bfloat16)
        return accum + jnp.einsum(
            "mhqk,mkhd->mqhd",
            probs_low,
            span_slice(value_heads, block, 1),
            preferred_element_type=jnp.float32,
        )

    attn_acc = lax.fori_loop(
        0, block_count, value_step, jnp.zeros((batches, block_rows, local_heads, HD), jnp.float32)
    )
    attn_low = attn_acc.reshape(all_rows, local_width).astype(jnp.bfloat16)
    attn_out = lax.psum(jnp.dot(attn_low, out_full, preferred_element_type=jnp.float32), "tp")
    middle = inputs + attn_out
    second_out, second_hat, second_recip = layer_norm(middle, ln2_gain, ln2_bias)
    second_low = second_out.astype(jnp.bfloat16)
    up_full = jnp.dot(second_low, up_full_w, preferred_element_type=jnp.float32)
    rectified = jnp.maximum(up_full, 0.0)
    act_low = (rectified * rectified).astype(jnp.bfloat16)
    ffn_out = lax.psum(jnp.dot(act_low, down_full_w, preferred_element_type=jnp.float32), "tp")
    result = (middle + ffn_out).reshape(batches, block_rows, model_width).astype(jnp.bfloat16)
    grad_out = (
        cotangent.astype(jnp.float32) * token_valid[:, :, None].astype(jnp.float32)
    ).reshape(all_rows, model_width)
    grad_low = grad_out.astype(jnp.bfloat16)
    down_wgrad = jnp.einsum("tf,td->fd", act_low, grad_low, preferred_element_type=jnp.float32)
    act_grad = jnp.einsum("td,fd->tf", grad_low, down_full_w, preferred_element_type=jnp.float32)
    up_grad_low = (act_grad * 2.0 * rectified).astype(jnp.bfloat16)
    up_wgrad = jnp.einsum("td,tf->df", second_low, up_grad_low, preferred_element_type=jnp.float32)
    second_grad = lax.psum(
        jnp.einsum("tf,df->td", up_grad_low, up_full_w, preferred_element_type=jnp.float32), "tp"
    )
    gain_two_grad = jnp.sum(second_grad * second_hat, axis=0)
    bias_two_grad = jnp.sum(second_grad, axis=0)
    middle_grad = grad_out + norm_back(second_grad, second_hat, second_recip, ln2_gain)
    middle_low = middle_grad.astype(jnp.bfloat16)
    out_wgrad = jnp.einsum("tn,td->nd", attn_low, middle_low, preferred_element_type=jnp.float32)
    attn_flat = jnp.einsum(
        "td,nd->tn", middle_low, out_full, preferred_element_type=jnp.float32
    ).astype(jnp.bfloat16)
    attn_grad = attn_flat.reshape(batches, block_rows, local_heads, HD)

    def delta_step(block, accum):
        key_pos = block * key_span + span_iota
        probs_full = jnp.exp(
            tile_scores(query_heads, span_slice(key_heads, block, 1), positions, key_pos, lengths)
            - log_total
        )
        prob_grad = jnp.einsum(
            "mqhd,mkhd->mhqk",
            attn_grad,
            span_slice(value_heads, block, 1),
            preferred_element_type=jnp.float32,
        )
        return accum + jnp.sum(probs_full * prob_grad, axis=-1, keepdims=True)

    delta = lax.fori_loop(0, block_count, delta_step, jnp.zeros(stat_shape, jnp.float32))
    query_zero = jnp.zeros((batches, block_rows, local_heads, HD), jnp.float32)

    def back_step(block, carry):
        accum, buffer = carry
        key_pos = block * key_span + span_iota
        key_part = span_slice(key_heads, block, 1)
        probs_full, prob_grad, score_grad = tile_grads(
            query_heads,
            key_part,
            span_slice(value_heads, block, 1),
            attn_grad,
            log_total,
            delta,
            positions,
            key_pos,
            lengths,
        )
        probs_again = probs_full.astype(jnp.bfloat16)
        accum = (
            accum
            + jnp.einsum(
                "mhqk,mkhd->mqhd", score_grad, key_part, preferred_element_type=jnp.float32
            )
            * SCALING
        )
        key_term = (
            jnp.einsum(
                "mhqk,mqhd->mkhd", score_grad, query_heads, preferred_element_type=jnp.float32
            )
            * SCALING
        )
        value_term = jnp.einsum(
            "mhqk,mqhd->mkhd", probs_again, attn_grad, preferred_element_type=jnp.float32
        )
        stacked = jnp.stack(
            [
                key_term.reshape(batches, key_span, local_width),
                value_term.reshape(batches, key_span, local_width),
            ],
            axis=2,
        )
        buffer = lax.dynamic_update_slice_in_dim(buffer, stacked, block * key_span, 1)
        return (accum, buffer)

    buffer_zero = jnp.zeros((batches, slot_span, 2, local_width), jnp.float32)
    query_grad, pair_terms = lax.fori_loop(0, block_count, back_step, (query_zero, buffer_zero))
    pair_grad = lax.psum_scatter(pair_terms, "ctx", scatter_dimension=1, tiled=True)
    mixed_grad = jnp.concatenate(
        [query_grad.reshape(batches, block_rows, 1, local_width), pair_grad], axis=2
    )
    later = shifted(mixed_grad[:, :2], "ctx", -1)
    ahead = jnp.concatenate([mixed_grad, later], axis=1)
    pre_grad = (
        conv_kernel[0] * ahead[:, :block_rows]
        + conv_kernel[1] * ahead[:, 1 : block_rows + 1]
        + conv_kernel[2] * ahead[:, 2:]
    ).astype(jnp.bfloat16)
    kernel_grad = jnp.stack(
        [
            jnp.sum(extended[:, 2 - offset : 2 - offset + block_rows] * mixed_grad, axis=(0, 1))
            for offset in range(3)
        ]
    )
    shift_grad = jnp.sum(mixed_grad, axis=(0, 1))
    pre_grad = pre_grad.reshape(all_rows, 3, local_width)
    qkv_wgrad = jnp.einsum("td,tcn->dcn", first_low, pre_grad, preferred_element_type=jnp.float32)
    first_grad = lax.psum(
        jnp.einsum("tcn,dcn->td", pre_grad, qkv_full, preferred_element_type=jnp.float32), "tp"
    )
    gain_one_grad = jnp.sum(first_grad * first_hat, axis=0)
    bias_one_grad = jnp.sum(first_grad, axis=0)
    input_grad = middle_grad + norm_back(first_grad, first_hat, first_recip, ln1_gain)
    input_grad = input_grad.reshape(batches, block_rows, model_width)
    summed = lax.psum(
        (
            qkv_wgrad,
            out_wgrad,
            up_wgrad,
            down_wgrad,
            gain_one_grad,
            bias_one_grad,
            kernel_grad,
            shift_grad,
            gain_two_grad,
            bias_two_grad,
        ),
        ("fsdp", "ctx"),
    )
    share_rows = model_width // lax.axis_size("fsdp")
    owner_start = lax.axis_index("fsdp") * share_rows
    qkv_share = lax.dynamic_slice_in_dim(summed[0], owner_start, share_rows, 0)
    out_share = lax.dynamic_slice_in_dim(summed[1], owner_start, share_rows, 1)
    up_share = lax.dynamic_slice_in_dim(summed[2], owner_start, share_rows, 0)
    down_share = lax.dynamic_slice_in_dim(summed[3], owner_start, share_rows, 1)
    small_sums = summed[4:]
    return (
        result,
        input_grad,
        small_sums[0],
        small_sums[1],
        qkv_share,
        small_sums[2],
        small_sums[3],
        out_share,
        small_sums[4],
        small_sums[5],
        up_share,
        down_share,
    )


def solution(mesh):
    placed = (
        P("fsdp", "ctx", None),
        P("fsdp"),
        P("fsdp", "ctx", None),
        P(),
        P(),
        P("fsdp", None, "tp"),
        P(None, None, "tp"),
        P(None, "tp"),
        P("tp", "fsdp"),
        P(),
        P(),
        P("fsdp", "tp"),
        P("tp", "fsdp"),
    )
    return jax.shard_map(
        local,
        mesh=mesh,
        in_specs=placed,
        out_specs=(
            P("fsdp", "ctx", None),
            P("fsdp", "ctx", None),
            P(),
            P(),
            P("fsdp", None, "tp"),
            P(None, None, "tp"),
            P(None, "tp"),
            P("tp", "fsdp"),
            P(),
            P(),
            P("fsdp", "tp"),
            P("tp", "fsdp"),
        ),
        check_vma=False,
    )
```

profile of v0, /device:TPU:0, one launch (start us, length us, event | category | flops | bytes accessed | tf_op | source)
XLA Modules:
  0.0 899.5 jit_solution(3532479969276561310)
XLA Ops:
  11.3 33.8 %all-gather.5.cloned.1.call-done = bf16[768,3,384]{2,0,1:T(8,128)(2,1)} async-done(((bf16[192,3,384]{2,0,1:T(8,128)(2,1)}), bf16[768,3,384]{2,0,1:T(8,128)(2,1)}) %all-gather.5.cloned.1.call-update) | async-done | bytes 1769488 | tf_op jit(solution)/shard_map/all_gather | solution.py:76
  56.9 11.0 %all_gather.17 = bf16[384,768]{0,1:T(8,128)(2,1)S(1)} all-gather(bf16[384,192]{0,1:T(8,128)(2,1)S(1)} %copy-done.26), channel_id=1, replica_groups=mesh['fsdp'=4,'ctx'=4,'tp'=2] {'fsdp'}, dimensions={1}, use_global_device_ids=true | all-gather | bytes 737280 | tf_op jit(solution)/shard_map/all_gather | solution.py:77
  68.0 53.2 %all-gather.7.cloned.1.call-done = bf16[2,1024,2,384]{1,3,0,2:T(8,128)(2,1)} async-done(((bf16[2,256,2,384]{1,3,0,2:T(8,128)(2,1)}), bf16[2,1024,2,384]{1,3,0,2:T(8,128)(2,1)}) %all-gather.7.cloned.1.call-update) | async-done | bytes 3145744 | tf_op jit(solution)/shard_map/all_gather | solution.py:113
  124.6 6.7 while.48
  132.2 8.3 while.49
  133.0 7.6 fusion.144
  147.7 15.0 %all-reduce.8.cloned.1.call-done = f32[512,768]{1,0:T(8,128)} async-done(((f32[512,768]{1,0:T(8,128)}), f32[512,768]{1,0:T(8,128)}) %all-reduce.8.cloned.1.call-update) | async-done | bytes 1572880 | tf_op jit(solution)/shard_map/psum | solution.py:155
  164.9 38.1 %all-gather.9.cloned.1.call-done = bf16[768,1536]{1,0:T(8,128)(2,1)} async-done(((bf16[192,1536]{1,0:T(8,128)(2,1)}), bf16[768,1536]{1,0:T(8,128)(2,1)}) %all-gather.9.cloned.1.call-update) | async-done | bytes 2359312 | tf_op jit(solution)/shard_map/all_gather | solution.py:78
  203.0 4.8 convolution_maximum_fusion
  207.8 34.2 %all-gather.11.cloned.1.call-done = bf16[1536,768]{0,1:T(8,128)(2,1)} async-done(((bf16[1536,192]{0,1:T(8,128)(2,1)}), bf16[1536,768]{0,1:T(8,128)(2,1)}) %all-gather.11.cloned.1.call-update) | async-done | bytes 2359312 | tf_op jit(solution)/shard_map/all_gather | solution.py:79
  250.5 20.2 %all-reduce.10.cloned.1.call-done = f32[512,768]{1,0:T(8,128)} async-done(((f32[512,768]{1,0:T(8,128)}), f32[512,768]{1,0:T(8,128)}) %all-reduce.10.cloned.1.call-update) | async-done | bytes 1572880 | tf_op jit(solution)/shard_map/psum | solution.py:172
  277.0 14.6 %while.50 = (s32[]{:T(128)}, f32[2,6,256,1]{2,0,1,3:T(2,128)S(1)}, s32[]{:T(128)}, s32[2]{0:T(128)S(1)}, bf16[2,256,6,64]{1,3,2,0:T(8,128)(2,1)S(1)}, /*index=5*...) while((s32[]{:T(128)}, f32[2,6,256,1]{2,0,1,3:T(2,128)S(1)}, ...), condition=%wide.region_17.18_spmd.clone, body=%wide.region_15.17_spmd.clone.sunk | while | flops 821824768 | bytes 37042356 | solution.py:199
  277.0 6.3 fusion.149
  283.9 7.7 multiply_reduce_fusion.10
  295.2 25.8 %while.51 = (s32[]{:T(128)}, f32[2,256,6,64]{1,3,2,0:T(8,128)S(1)}, f32[2,1024,2,384]{1,3,0,2:T(8,128)}, s32[]{:T(128)}, s32[2]{0:T(128)S(1)}, /*index=5*/bf16[2...) while((s32[]{:T(128)}, f32[2,256,6,64]{1,3,2,0:T(8,128)S(1)}, ...), condition=%wide.region_19.20_spmd.clone, body=%wide.region_18.19_spmd.clone.sunk | while | flops 2048265472 | bytes 123263216 | solution.py:245
  295.6 6.3 fusion.160
  302.6 8.4 multiply_convert_fusion.5
  321.1 112.1 %reduce-scatter.2.cloned.1.call-done = f32[2,256,2,384]{1,3,0,2:T(8,128)} async-done(((f32[2,1024,2,384]{1,3,0,2:T(8,128)}), f32[2,256,2,384]{1,3,0,2:T(8,128)}) %reduce-scatter.2.cloned.1.call-update) | async-done | bytes 1572880 | tf_op jit(solution)/shard_map/reduce_scatter | solution.py:246
  436.2 5.3 fusion.66
  445.3 4.6 multiply_reduce_fusion.3
  456.9 5.3 fusion.72
  471.0 10.6 %all-reduce.14.cloned.1.call-done = (f32[512,768]{1,0:T(8,128)}, f32[512,768]{1,0:T(8,128)}) async-done(((f32[512,768]{1,0:T(8,128)}, f32[512,768]{1,0:T(8,128)}), (f32[512,768]{1,0:T(8,128)}, f32[512,768]{1,0:T(8,128)})) %all-reduce.14.cloned.1.call-update) | async-done | bytes 3145744 | tf_op jit(solution)/shard_map/psum | solution.py:162
  483.8 82.5 %all-reduce = (f32[768]{0:T(1024)}, f32[768]{0:T(1024)}, f32[3,3,384]{2,1,0:T(4,128)}, f32[3,384]{1,0:T(4,128)}, f32[768]{0:T(1024)}, /*index=5*/f32[768]{0:T(1024)}) all-reduce(f32[768]{0:T(1024)S(1)} %get-tuple-element.486, f32[768]{0:T(1024)S(1)} %get-tuple-element.492, ...), channel_id=1, replica_groups=mesh['fsdp'=4,'ctx'=4,'tp'=2] {'fsdp','ctx'}, use_global_device_ids=true, to_apply=%region_25.26 | all-reduce | flops 7680 | bytes 61440 | tf_op jit(solution)/shard_map/psum | solution.py:273
  570.6 313.6 %all-reduce.12.cloned.1.call-done = (f32[768,3,384]{2,0,1:T(8,128)}, f32[384,768]{0,1:T(8,128)}, f32[768,1536]{1,0:T(8,128)}, f32[1536,768]{0,1:T(8,128)}) async-done(((f32[768,3,384]{2,0,1:T(8,128)}, f32[384,768]{0,1:T(8,128)}, f32[768,1536]{1,0:T(8,128)}, f32[1536,768]{0,1:T(8,128)}), (f32[768,3,384]{2,0,1:T(8,128)}, f32[384,768]{0,1:T(8,128)}, f32[768,1536]{1,0:T(8,128)}, ...) | async-done | bytes 14155792 | tf_op jit(solution)/shard_map/psum | solution.py:273
  (244 shorter events, 103.1 us)
Async XLA Ops:
  7.2 37.9 %all-gather.5.cloned.1.call-start = ((), (), s32[]{:S(2)}) async-start(), calls=%async_computation.1 | async-start | bytes 2211840 | tf_op jit(solution)/shard_map/all_gather | solution.py:76
  7.9 113.2 %all-gather.7.cloned.1.call-start = ((), (), s32[]{:S(2)}) async-start(), calls=%async_computation.2 | async-start | bytes 3932160 | tf_op jit(solution)/shard_map/all_gather | solution.py:113
  11.3 39.9 %copy-start.43 = (f32[3,3,384]{2,1,0:T(4,128)S(1)}, f32[3,3,384]{2,1,0:T(4,128)}, u32[]{:S(2)}) copy-start(f32[3,3,384]{2,1,0:T(4,128)} %param.27) | copy-start | bytes 41476
  47.8 4.8 collective-permute-start
  55.8 12.1 %copy-start = (bf16[2,256,3,384]{1,3,0,2:T(8,128)(2,1)}, bf16[2,256,3,384]{1,3,0,2:T(8,128)(2,1)S(1)}, u32[]{:S(2)}) copy-start(bf16[2,256,3,384]{1,3,0,2:T(8,128)(2,1)S(1)} %add_convert_fusion) | copy-start | bytes 3538948
  56.8 105.9 %all-reduce.8.cloned.1.call-start = ((), (), s32[]{:S(2)}) async-start(), calls=%async_computation.3 | async-start | bytes 3145728 | tf_op jit(solution)/shard_map/psum | solution.py:155
  68.0 74.3 %copy-start.16 = (bf16[384,768]{0,1:T(8,128)(2,1)}, bf16[384,768]{0,1:T(8,128)(2,1)S(1)}, u32[]{:S(2)}) copy-start(bf16[384,768]{0,1:T(8,128)(2,1)S(1)} %all_gather.17) | copy-start | bytes 1769476
  68.0 56.6 %copy-start.25 = (s32[2]{0:T(128)S(1)}, s32[2]{0:T(128)}, u32[]{:S(2)}) copy-start(s32[2]{0:T(128)} %param.22) | copy-start | bytes 28
  144.1 58.9 %all-gather.9.cloned.1.call-start = ((), (), s32[]{:S(2)}) async-start(), calls=%async_computation.4 | async-start | bytes 2949120 | tf_op jit(solution)/shard_map/all_gather | solution.py:78
  144.6 97.4 %all-gather.11.cloned.1.call-start = ((), (), s32[]{:S(2)}) async-start(), calls=%async_computation.5 | async-start | bytes 2949120 | tf_op jit(solution)/shard_map/all_gather | solution.py:79
  145.2 125.5 %all-reduce.10.cloned.1.call-start = ((), (), s32[]{:S(2)}) async-start(), calls=%async_computation.6 | async-start | bytes 3145728 | tf_op jit(solution)/shard_map/psum | solution.py:172
  164.6 109.0 %copy-start.3 = (f32[512,768]{1,0:T(8,128)}, f32[512,768]{1,0:T(8,128)S(1)}, u32[]{:S(2)}) copy-start(f32[512,768]{1,0:T(8,128)S(1)} %get-tuple-element.584) | copy-start | bytes 4718596
  164.6 38.4 %copy-start.48 = (f32[768]{0:T(1024)S(1)}, f32[768]{0:T(1024)}, u32[]{:S(2)}) copy-start(f32[768]{0:T(1024)} %param.30) | copy-start | bytes 9220
  164.6 109.0 %copy-start.39 = (f32[512]{0:T(512)}, f32[512]{0:T(512)S(1)}, u32[]{:S(2)}) copy-start(f32[512]{0:T(512)S(1)} %broadcast_multiply_fusion.4) | copy-start | bytes 6148
  164.9 108.7 %copy-start.41 = (f32[512]{0:T(512)}, f32[512]{0:T(512)S(1)}, u32[]{:S(2)}) copy-start(f32[512]{0:T(512)S(1)} %add_rsqrt_fusion) | copy-start | bytes 6148
  250.2 183.0 %reduce-scatter.2.cloned.1.call-start = ((), (), s32[]{:S(2)}) async-start(), calls=%async_computation.7 | async-start | bytes 7864320 | tf_op jit(solution)/shard_map/reduce_scatter | solution.py:246
  302.3 10.7 %slice-start = ((s8[12582912]{0:T(1024)(128)(4,1)}), s8[4194304]{0:T(1024)(128)(4,1)S(1)}, s32[]{:S(2)}) async-start(s8[12582912]{0:T(1024)(128)(4,1)} %bitcast.193), calls=%async_computation.10 | async-start | bytes 8388608 | tf_op jit(solution)/shard_map/while
  321.1 160.6 %all-reduce.14.cloned.1.call-start = ((), (), s32[]{:S(2)}) async-start(), calls=%async_computation.9 | async-start | bytes 6291456 | tf_op jit(solution)/shard_map/psum | solution.py:162
  434.7 6.8 collective-permute-start.1
  455.5 428.7 %all-reduce.12.cloned.1.call-start = ((), (), s32[]{:S(2)}) async-start(), calls=%async_computation.8 | async-start | bytes 28311552 | tf_op jit(solution)/shard_map/psum | solution.py:273
  470.9 10.7 %copy-start.36 = (f32[1,2,2,128]{3,1,2,0:T(2,128)S(1)}, f32[1,2,2,128]{3,1,2,0:T(2,128)}, u32[]{:S(2)}) copy-start(f32[1,2,2,128]{3,1,2,0:T(2,128)} %copy-done.35) | copy-start | bytes 6148
  470.9 10.7 %copy-start.38 = (f32[1,2,2,128]{3,1,2,0:T(2,128)S(1)}, f32[1,2,2,128]{3,1,2,0:T(2,128)}, u32[]{:S(2)}) copy-start(f32[1,2,2,128]{3,1,2,0:T(2,128)} %copy-done.37) | copy-start | bytes 6148
  471.0 12.9 %copy-start.44 = (f32[768]{0:T(1024)S(1)}, f32[768]{0:T(1024)}, u32[]{:S(2)}) copy-start(f32[768]{0:T(1024)} %get-tuple-element.484) | copy-start | bytes 9220
  471.0 12.9 %copy-start.45 = (f32[768]{0:T(1024)S(1)}, f32[768]{0:T(1024)}, u32[]{:S(2)}) copy-start(f32[768]{0:T(1024)} %get-tuple-element.491) | copy-start | bytes 9220
  (50 other events, 142.4 us)
Sparse Core Ops, SparseCore 0:
  9.9 35.1 all-gather.4
  56.9 64.1 all-gather.6
  144.2 18.5 all-reduce.7
  164.4 38.5 all-gather.8
  204.7 37.3 all-gather.10
  250.3 20.3 all-reduce.9
  321.2 111.9 reduce-scatter.1
  455.7 25.9 all-reduce.13
  488.6 395.5 all-reduce.11
where the time goes:
time: 907 us; the launch traced here: 900 us
  waiting for transfers between devices  633 us (70%)
  blocking collectives  93.5 us (10%)
  matrix products  85.2 us (9%)
  other arithmetic  36.6 us (4%)
  local copies, waits for them, and re-layouts  29.8 us (3%)
  between operations  14.8 us (2%)
    psum x1, waiting for transfers between devices, local(): lax.psum((qkv_wgrad, out_wgrad, up_wgrad, down_wgrad, gain_one_grad, bias...  314 us
    reduce_scatter x1, waiting for transfers between devices, local(): lax.psum_scatter(pair_terms, 'ctx', scatter_dimension=1, tiled=True)  112 us
    psum x1, blocking collectives, local(): lax.psum((qkv_wgrad, out_wgrad, up_wgrad, down_wgrad, gain_one_grad, bias...  82.5 us
    all_gather x1, waiting for transfers between devices, local(): whole_pairs = lax.all_gather(own_pairs, 'ctx', axis=1, tiled=True)  53.2 us
    all_gather x1, waiting for transfers between devices, local(): lax.all_gather(up_weight, 'fsdp', axis=0, tiled=True)  38.1 us
    all_gather x1, waiting for transfers between devices, local(): lax.all_gather(down_weight, 'fsdp', axis=1, tiled=True)  34.2 us
    all_gather x1, waiting for transfers between devices, local(): lax.all_gather(qkv_weight, 'fsdp', axis=0, tiled=True)  33.8 us
    psum x1, waiting for transfers between devices, local(): lax.psum(jnp.einsum('tf,df->td', up_grad_low, up_full_w, preferred_elemen...  20.2 us
  transfers between devices with their start and end apart: 11, of which 10 were waited for; matrix products, arithmetic and copies ran while one was open for 4% of the time, Pallas kernels for 0%

commit v1 on v0

--- a/solution.py
+++ b/solution.py
@@ -270,12 +270,18 @@
     bias_one_grad = jnp.sum(first_grad, axis=0)
     input_grad = middle_grad + norm_back(first_grad, first_hat, first_recip, ln1_gain)
     input_grad = input_grad.reshape(batches, block_rows, model_width)
-    summed = lax.psum(
+    def owned(term, axis_pos):
+        part = lax.psum_scatter(
+            term.astype(jnp.bfloat16), "fsdp", scatter_dimension=axis_pos, tiled=True
+        )
+        return lax.psum(part, "ctx").astype(jnp.float32)
+
+    qkv_share = owned(qkv_wgrad, 0)
+    out_share = owned(out_wgrad, 1)
+    up_share = owned(up_wgrad, 0)
+    down_share = owned(down_wgrad, 1)
+    small_sums = lax.psum(
         (
-            qkv_wgrad,
-            out_wgrad,
-            up_wgrad,
-            down_wgrad,
             gain_one_grad,
             bias_one_grad,
             kernel_grad,
@@ -285,13 +291,6 @@
         ),
         ("fsdp", "ctx"),
     )
-    share_rows = model_width // lax.axis_size("fsdp")
-    owner_start = lax.axis_index("fsdp") * share_rows
-    qkv_share = lax.dynamic_slice_in_dim(summed[0], owner_start, share_rows, 0)
-    out_share = lax.dynamic_slice_in_dim(summed[1], owner_start, share_rows, 1)
-    up_share = lax.dynamic_slice_in_dim(summed[2], owner_start, share_rows, 0)
-    down_share = lax.dynamic_slice_in_dim(summed[3], owner_start, share_rows, 1)
-    small_sums = summed[4:]
     return (
         result,
         input_grad,

time: 907 us -> 700 us (0.77)
  waiting for transfers between devices: 633 us -> 438 us
  matrix products: 85.2 us -> 71.5 us
    psum x1, waiting for transfers between devices: 314 us -> 0.01 us  [owned(): return lax.psum(part, 'ctx').astype(jnp.float32)]
    reduce_scatter x0 -> x4, waiting for transfers between devices: none -> 112 us  [owned(): lax.psum_scatter(term.astype(jnp.bfloat16), 'fsdp', scatter_dimension=axi...]
    psum x1, waiting for transfers between devices: 10.6 us -> 26.1 us  [local(): lax.psum(jnp.dot(act_low, down_full_w, preferred_element_type=jnp.float32...]
    reduce_scatter x1, waiting for transfers between devices: 112 us -> 98 us  [local(): lax.psum_scatter(pair_terms, 'ctx', scatter_dimension=1, tiled=True)]
  transfers between devices with their start and end apart: 11 -> 15, of which waited for: 10 -> 13; matrix products, arithmetic and copies ran while one was open for 4% -> 8% of each run, Pallas kernels for 0% -> 0%
where the time goes in v1:
time: 700 us; the launch traced here: 693 us
  waiting for transfers between devices  438 us (63%)
  blocking collectives  92.9 us (13%)
  matrix products  71.5 us (10%)
  other arithmetic  43.9 us (6%)
  local copies, waits for them, and re-layouts  25.1 us (4%)
  between operations  15 us (2%)
    reduce_scatter x4, waiting for transfers between devices, owned(): lax.psum_scatter(term.astype(jnp.bfloat16), 'fsdp', scatter_dimension=axi...  112 us
    reduce_scatter x1, waiting for transfers between devices, local(): lax.psum_scatter(pair_terms, 'ctx', scatter_dimension=1, tiled=True)  98 us
    psum x1, blocking collectives, local(): lax.psum((gain_one_grad, bias_one_grad, kernel_grad, shift_grad, gain_two...  81.9 us
    all_gather x1, waiting for transfers between devices, local(): whole_pairs = lax.all_gather(own_pairs, 'ctx', axis=1, tiled=True)  53.2 us
    all_gather x1, waiting for transfers between devices, local(): lax.all_gather(up_weight, 'fsdp', axis=0, tiled=True)  38.1 us
    all_gather x1, waiting for transfers between devices, local(): lax.all_gather(qkv_weight, 'fsdp', axis=0, tiled=True)  34.4 us
    all_gather x1, waiting for transfers between devices, local(): lax.all_gather(down_weight, 'fsdp', axis=1, tiled=True)  34.1 us
    psum x1, waiting for transfers between devices, local(): lax.psum(jnp.dot(act_low, down_full_w, preferred_element_type=jnp.float32...  26.1 us
  transfers between devices with their start and end apart: 15, of which 13 were waited for; matrix products, arithmetic and copies ran while one was open for 8% of the time, Pallas kernels for 0%

profile of v1, /device:TPU:0, one launch (start us, length us, event | category | flops | bytes accessed | tf_op | source)
XLA Modules:
  0.0 692.7 jit_solution(6675761201139919809)
XLA Ops:
  10.7 34.4 %all-gather.5.cloned.1.call-done = bf16[768,3,384]{2,0,1:T(8,128)(2,1)} async-done(((bf16[192,3,384]{2,0,1:T(8,128)(2,1)}), bf16[768,3,384]{2,0,1:T(8,128)(2,1)}) %all-gather.5.cloned.1.call-update) | async-done | bytes 1769488 | tf_op jit(solution)/shard_map/all_gather | solution.py:76
  56.9 11.0 %all_gather.17 = bf16[384,768]{0,1:T(8,128)(2,1)S(1)} all-gather(bf16[384,192]{0,1:T(8,128)(2,1)S(1)} %copy-done.29), channel_id=1, replica_groups=mesh['fsdp'=4,'ctx'=4,'tp'=2] {'fsdp'}, dimensions={1}, use_global_device_ids=true | all-gather | bytes 737280 | tf_op jit(solution)/shard_map/all_gather | solution.py:77
  68.0 53.2 %all-gather.7.cloned.1.call-done = bf16[2,1024,2,384]{1,3,0,2:T(8,128)(2,1)} async-done(((bf16[2,256,2,384]{1,3,0,2:T(8,128)(2,1)}), bf16[2,1024,2,384]{1,3,0,2:T(8,128)(2,1)}) %all-gather.7.cloned.1.call-update) | async-done | bytes 3145744 | tf_op jit(solution)/shard_map/all_gather | solution.py:113
  124.7 6.7 while.48
  132.3 8.4 %while.49 = (s32[]{:T(128)}, f32[2,256,6,64]{1,3,2,0:T(8,128)}, s32[]{:T(128)}, s32[2]{0:T(128)S(1)}, bf16[2,256,6,64]{1,3,2,0:T(8,128)(2,1)S(1)}, /*index=5*/bf...) while((s32[]{:T(128)}, f32[2,256,6,64]{1,3,2,0:T(8,128)}, ...), condition=%wide.region_7.8_spmd.clone, body=%wide.region_6.7_spmd.clone.sunk | while | flops 818875648 | bytes 6715529 | solution.py:151
  133.2 7.6 %fusion.141 = f32[2,256,6,64]{1,3,2,0:T(8,128)} fusion(f32[2,256,6,64]{1,3,2,0:T(8,128)} %get-tuple-element.885, bf16[2,1024,6,64]{1,3,2,0:T(8,128)(2,1)} %get-tuple-element.902, f32[2,6,256]{2,1,0:T(8,128)S(1)} %bitcast.217, pred[2,256,1024]{2,1,0:T(8,128)(4,1)S(1)} %broadcast_and_fusion.9, bf16[2,256,6,64]{1,3,2,0:T(8,128)(2,1)S(1)} %get-tuple-element.899, ...), kind=kOutput, calls=%fused_computation.23.clone.1 | convolution fusion | flops 818085888 | bytes 5648384 | tf_op jit(solution)/shard_map/while/body/mhqk,mkhd->mqhd/dot_general | solution.py:144
  148.0 15.0 %all-reduce.8.cloned.1.call-done = f32[512,768]{1,0:T(8,128)} async-done(((f32[512,768]{1,0:T(8,128)}), f32[512,768]{1,0:T(8,128)}) %all-reduce.8.cloned.1.call-update) | async-done | bytes 1572880 | tf_op jit(solution)/shard_map/psum | solution.py:155
  165.2 38.1 %all-gather.9.cloned.1.call-done = bf16[768,1536]{1,0:T(8,128)(2,1)} async-done(((bf16[192,1536]{1,0:T(8,128)(2,1)}), bf16[768,1536]{1,0:T(8,128)(2,1)}) %all-gather.9.cloned.1.call-update) | async-done | bytes 2359312 | tf_op jit(solution)/shard_map/all_gather | solution.py:78
  203.3 4.9 convolution_maximum_fusion
  208.2 34.1 %all-gather.11.cloned.1.call-done = bf16[1536,768]{0,1:T(8,128)(2,1)} async-done(((bf16[1536,192]{0,1:T(8,128)(2,1)}), bf16[1536,768]{0,1:T(8,128)(2,1)}) %all-gather.11.cloned.1.call-update) | async-done | bytes 2359312 | tf_op jit(solution)/shard_map/all_gather | solution.py:79
  251.2 19.9 %all-reduce.10.cloned.1.call-done = f32[512,768]{1,0:T(8,128)} async-done(((f32[512,768]{1,0:T(8,128)}), f32[512,768]{1,0:T(8,128)}) %all-reduce.10.cloned.1.call-update) | async-done | bytes 1572880 | tf_op jit(solution)/shard_map/psum | solution.py:172
  277.0 7.2 %while.50 = (s32[]{:T(128)}, f32[2,6,256,1]{2,0,1,3:T(2,128)S(1)}, s32[]{:T(128)}, s32[2]{0:T(128)S(1)}, bf16[2,256,6,64]{1,3,2,0:T(8,128)(2,1)S(1)}, /*index=5*...) while((s32[]{:T(128)}, f32[2,6,256,1]{2,0,1,3:T(2,128)S(1)}, ...), condition=%wide.region_17.18_spmd.clone, body=%wide.region_15.17_spmd.clone.sunk | while | flops 821824768 | bytes 37042348 | solution.py:199
  279.4 4.7 multiply_reduce_fusion.10
  288.5 19.0 %while.51 = (s32[]{:T(128)}, f32[2,256,6,64]{1,3,2,0:T(8,128)S(1)}, f32[2,1024,2,384]{1,3,0,2:T(8,128)}, s32[]{:T(128)}, s32[2]{0:T(128)S(1)}, /*index=5*/bf16[2...) while((s32[]{:T(128)}, f32[2,256,6,64]{1,3,2,0:T(8,128)S(1)}, ...), condition=%wide.region_19.20_spmd.clone, body=%wide.region_18.19_spmd.clone.sunk | while | flops 2048265472 | bytes 87087288 | solution.py:245
  294.5 6.5 multiply_convert_fusion.5
  310.5 4.9 convolution_convert_fusion
  321.6 98.0 %reduce-scatter.6.cloned.1.call-done = f32[2,256,2,384]{1,3,0,2:T(8,128)} async-done(((f32[2,1024,2,384]{1,3,0,2:T(8,128)}), f32[2,256,2,384]{1,3,0,2:T(8,128)}) %reduce-scatter.6.cloned.1.call-update) | async-done | bytes 1572880 | tf_op jit(solution)/shard_map/reduce_scatter | solution.py:246
  433.9 4.5 multiply_reduce_fusion.3
  442.2 5.4 fusion.65
  453.4 36.1 %reduce-scatter.14.cloned.1.call-done = bf16[1536,192]{0,1:T(8,128)(2,1)} async-done(((bf16[1536,768]{0,1:T(8,128)(2,1)}), bf16[1536,192]{0,1:T(8,128)(2,1)}) %reduce-scatter.14.cloned.1.call-update) | async-done | bytes 589840 | tf_op jit(solution)/shard_map/reduce_scatter | solution.py:274
  489.5 40.3 %reduce-scatter.12.cloned.1.call-done = bf16[192,1536]{1,0:T(8,128)(2,1)} async-done(((bf16[768,1536]{1,0:T(8,128)(2,1)}), bf16[192,1536]{1,0:T(8,128)(2,1)}) %reduce-scatter.12.cloned.1.call-update) | async-done | bytes 589840 | tf_op jit(solution)/shard_map/reduce_scatter | solution.py:274
  529.8 35.6 %reduce-scatter.8.cloned.1.call-done = bf16[192,3,384]{2,0,1:T(8,128)(2,1)} async-done(((bf16[768,3,384]{2,0,1:T(8,128)(2,1)}), bf16[192,3,384]{2,0,1:T(8,128)(2,1)}) %reduce-scatter.8.cloned.1.call-update) | async-done | bytes 442384 | tf_op jit(solution)/shard_map/reduce_scatter | solution.py:274
  565.4 26.1 %all-reduce.12.cloned.1.call-done = (f32[512,768]{1,0:T(8,128)}, f32[512,768]{1,0:T(8,128)}) async-done(((f32[512,768]{1,0:T(8,128)}, f32[512,768]{1,0:T(8,128)}), (f32[512,768]{1,0:T(8,128)}, f32[512,768]{1,0:T(8,128)})) %all-reduce.12.cloned.1.call-update) | async-done | bytes 3145744 | tf_op jit(solution)/shard_map/psum | solution.py:162
  593.7 81.9 %all-reduce = (f32[768]{0:T(1024)}, f32[768]{0:T(1024)}, f32[3,3,384]{2,1,0:T(4,128)}, f32[3,384]{1,0:T(4,128)}, f32[768]{0:T(1024)}, /*index=5*/f32[768]{0:T(1024)}) all-reduce(f32[768]{0:T(1024)S(1)} %get-tuple-element.486, f32[768]{0:T(1024)S(1)} %get-tuple-element.492, ...), channel_id=1, replica_groups=mesh['fsdp'=4,'ctx'=4,'tp'=2] {'fsdp','ctx'}, use_global_device_ids=true, to_apply=%region_25.26 | all-reduce | flops 7680 | bytes 61440 | tf_op jit(solution)/shard_map/psum | solution.py:283
  (261 shorter events, 115.0 us)
Async XLA Ops:
  7.2 37.9 %all-gather.5.cloned.1.call-start = ((), (), s32[]{:S(2)}) async-start(), calls=%async_computation.5 | async-start | bytes 2211840 | tf_op jit(solution)/shard_map/all_gather | solution.py:76
  7.9 113.2 %all-gather.7.cloned.1.call-start = ((), (), s32[]{:S(2)}) async-start(), calls=%async_computation.6 | async-start | bytes 3932160 | tf_op jit(solution)/shard_map/all_gather | solution.py:113
  47.8 4.8 collective-permute-start
  56.8 106.2 %all-reduce.8.cloned.1.call-start = ((), (), s32[]{:S(2)}) async-start(), calls=%async_computation.7 | async-start | bytes 3145728 | tf_op jit(solution)/shard_map/psum | solution.py:155
  68.0 74.4 %copy-start.15 = (bf16[384,768]{0,1:T(8,128)(2,1)}, bf16[384,768]{0,1:T(8,128)(2,1)S(1)}, u32[]{:S(2)}) copy-start(bf16[384,768]{0,1:T(8,128)(2,1)S(1)} %all_gather.17) | copy-start | bytes 1769476
  144.3 59.0 %all-gather.9.cloned.1.call-start = ((), (), s32[]{:S(2)}) async-start(), calls=%async_computation.8 | async-start | bytes 2949120 | tf_op jit(solution)/shard_map/all_gather | solution.py:78
  144.9 97.4 %all-gather.11.cloned.1.call-start = ((), (), s32[]{:S(2)}) async-start(), calls=%async_computation.9 | async-start | bytes 2949120 | tf_op jit(solution)/shard_map/all_gather | solution.py:79
  145.5 125.6 %all-reduce.10.cloned.1.call-start = ((), (), s32[]{:S(2)}) async-start(), calls=%async_computation.10 | async-start | bytes 3145728 | tf_op jit(solution)/shard_map/psum | solution.py:172
  164.8 109.1 %copy-start.3 = (f32[512,768]{1,0:T(8,128)}, f32[512,768]{1,0:T(8,128)S(1)}, u32[]{:S(2)}) copy-start(f32[512,768]{1,0:T(8,128)S(1)} %get-tuple-element.584) | copy-start | bytes 4718596
  164.9 109.1 %copy-start.42 = (f32[512]{0:T(512)}, f32[512]{0:T(512)S(1)}, u32[]{:S(2)}) copy-start(f32[512]{0:T(512)S(1)} %broadcast_multiply_fusion.4) | copy-start | bytes 6148
  165.2 108.8 %copy-start.47 = (f32[512]{0:T(512)}, f32[512]{0:T(512)S(1)}, u32[]{:S(2)}) copy-start(f32[512]{0:T(512)S(1)} %add_rsqrt_fusion) | copy-start | bytes 6148
  250.6 169.0 %reduce-scatter.6.cloned.1.call-start = ((), (), s32[]{:S(2)}) async-start(), calls=%async_computation.11 | async-start | bytes 7864320 | tf_op jit(solution)/shard_map/reduce_scatter | solution.py:246
  307.5 145.8 %reduce-scatter.10.cloned.1.call-start = ((), (), s32[]{:S(2)}) async-start(), calls=%async_computation.13 | async-start | bytes 737280 | tf_op jit(solution)/shard_map/reduce_scatter | solution.py:274
  310.4 179.1 %reduce-scatter.14.cloned.1.call-start = ((), (), s32[]{:S(2)}) async-start(), calls=%async_computation.15 | async-start | bytes 2949120 | tf_op jit(solution)/shard_map/reduce_scatter | solution.py:274
  315.4 214.4 %reduce-scatter.12.cloned.1.call-start = ((), (), s32[]{:S(2)}) async-start(), calls=%async_computation.14 | async-start | bytes 2949120 | tf_op jit(solution)/shard_map/reduce_scatter | solution.py:274
  321.6 243.7 %reduce-scatter.8.cloned.1.call-start = ((), (), s32[]{:S(2)}) async-start(), calls=%async_computation.12 | async-start | bytes 2211840 | tf_op jit(solution)/shard_map/reduce_scatter | solution.py:274
  423.5 5.7 collective-permute-start.1
  442.2 149.3 %all-reduce.12.cloned.1.call-start = ((), (), s32[]{:S(2)}) async-start(), calls=%async_computation.16 | async-start | bytes 6291456 | tf_op jit(solution)/shard_map/psum | solution.py:162
  453.2 112.1 %copy-start.44 = (f32[3,384]{1,0:T(4,128)S(1)}, f32[3,384]{1,0:T(4,128)}, u32[]{:S(2)}) copy-start(f32[3,384]{1,0:T(4,128)} %get-tuple-element.481) | copy-start | bytes 13828
  453.3 112.1 %copy-start.45 = (f32[3,384]{1,0:T(4,128)S(1)}, f32[3,384]{1,0:T(4,128)}, u32[]{:S(2)}) copy-start(f32[3,384]{1,0:T(4,128)} %get-tuple-element.482) | copy-start | bytes 13828
  453.3 112.1 %copy-start.46 = (f32[3,384]{1,0:T(4,128)S(1)}, f32[3,384]{1,0:T(4,128)}, u32[]{:S(2)}) copy-start(f32[3,384]{1,0:T(4,128)} %get-tuple-element.483) | copy-start | bytes 13828
  453.3 138.2 %copy-start.39 = (f32[1,2,2,128]{3,1,2,0:T(2,128)S(1)}, f32[1,2,2,128]{3,1,2,0:T(2,128)}, u32[]{:S(2)}) copy-start(f32[1,2,2,128]{3,1,2,0:T(2,128)} %copy-done.38) | copy-start | bytes 6148
  453.3 138.2 %copy-start.41 = (f32[1,2,2,128]{3,1,2,0:T(2,128)S(1)}, f32[1,2,2,128]{3,1,2,0:T(2,128)}, u32[]{:S(2)}) copy-start(f32[1,2,2,128]{3,1,2,0:T(2,128)} %copy-done.40) | copy-start | bytes 6148
  453.3 226.6 %all-reduce.14.cloned.1.call-start = ((), (), s32[]{:S(2)}) async-start(), calls=%async_computation.17 | async-start | bytes 3538944 | tf_op jit(solution)/shard_map/psum | solution.py:277
  (57 other events, 463.4 us)
Sparse Core Ops, SparseCore 0:
  9.9 35.1 all-gather.4
  57.0 64.1 all-gather.6
  144.4 18.5 all-reduce.7
  164.7 38.5 all-gather.8
  204.9 37.3 all-gather.10
  250.7 20.3 all-reduce.9
  307.6 111.9 reduce-scatter.5
  423.1 25.8 reduce-scatter.9
  452.1 37.3 reduce-scatter.13
  492.4 37.3 reduce-scatter.11
  532.8 32.4 reduce-scatter.7
  568.1 23.3 all-reduce.11
  594.2 78.6 all-reduce.13
